TPU v7x, 32 devices: a 4x4x1 block of a 4x4x8 slice. The times are simulated.
32 devices in a mesh: dp: 1 (over z), ep: 32 (over y, x, core).
Axes of the slice: x: 4, y: 4, z: 1, core: 2. Of those that a mesh axis runs over, the one named last changes fastest.
The devices are a block of a 4x4x8 slice.
Arguments:
- hidden: bfloat16 [32768, 2048], P(('dp', 'ep'))
- w_router: bfloat16 [2048, 64], replicated
- w_gate: bfloat16 [64, 2048, 1408], P('ep')
- w_up: bfloat16 [64, 2048, 1408], P('ep')
- w_down: bfloat16 [64, 1408, 2048], P('ep')
- shared_gate: bfloat16 [2048, 2816], replicated
- shared_up: bfloat16 [2048, 2816], replicated
- shared_down: bfloat16 [2816, 2048], replicated
- top_idx: int32 [32768, 6], P(('dp', 'ep'))
- keep_mask: int32 [32768, 6], P(('dp', 'ep'))
Outputs:
- output: bfloat16 [32768, 2048], P(('dp', 'ep'))
All inputs are finite; a program needn't handle non-finite values.
Results may differ from a plain program's by a relative error of at most 0.00690417.
Values are sent between devices in bfloat16 or wider.
A program may use at most 768 MiB of HBM per device.

v0:
```python
import jax
import jax.numpy as jnp
from jax import lax
from jax.sharding import PartitionSpec as P

ROUTE_SCALE = 16.0


def swiglu(tok_rows, gate_w, up_w, down_w):
    h_gate = jnp.dot(tok_rows, gate_w, preferred_element_type=jnp.float32)
    h_up = jnp.dot(tok_rows, up_w, preferred_element_type=jnp.float32)
    act_rows = (jax.nn.silu(h_gate) * h_up).astype(jnp.bfloat16)
    return jnp.dot(act_rows, down_w, preferred_element_type=jnp.float32)


def expert_bank(tok_rows, gate_w, up_w, down_w):
    h_gate = jnp.einsum("erd,edf->erf", tok_rows, gate_w, preferred_element_type=jnp.float32)
    h_up = jnp.einsum("erd,edf->erf", tok_rows, up_w, preferred_element_type=jnp.float32)
    act_rows = (jax.nn.silu(h_gate) * h_up).astype(jnp.bfloat16)
    return jnp.einsum("erf,efd->erd", act_rows, down_w, preferred_element_type=jnp.float32)


def route_gates(hidden, w_router, top_idx, keep_mask):
    logits = jnp.dot(hidden, w_router, preferred_element_type=jnp.float32)
    router_prob = jax.nn.softmax(logits, axis=-1)
    return ROUTE_SCALE * jnp.take_along_axis(router_prob, top_idx, axis=1) * keep_mask.astype(jnp.float32)


def solution(mesh):
    groups = mesh.shape["ep"]
    tok_spec = P(("dp", "ep"), None)
    bank_spec = P("ep", None, None)

    def device_fn(hidden, w_router, w_gate, w_up, w_down, shared_gate, shared_up, shared_down, top_idx, keep_mask):
        tokens, top_k = top_idx.shape
        hidden_dim = hidden.shape[1]
        experts = w_router.shape[1]
        per_dev = w_gate.shape[0]
        capacity = 8 * ((top_k * tokens + 4 * experts - 1) // (4 * experts))
        n_rows = experts * capacity
        gate_vals = route_gates(hidden, w_router, top_idx, keep_mask)
        pair_expert = top_idx.reshape(-1)
        pair_kept = keep_mask.reshape(-1) > 0
        onehot = ((pair_expert[:, None] == jnp.arange(experts)[None, :]) & pair_kept[:, None]).astype(jnp.int32)
        pair_slot = jnp.sum((jnp.cumsum(onehot, axis=0) - 1) * onehot, axis=1)
        dest_dev = pair_expert // per_dev
        local_exp = pair_expert % per_dev
        dest_row = jnp.where(pair_kept, (local_exp * groups + dest_dev) * capacity + pair_slot, n_rows)
        pair_token = jnp.arange(tokens * top_k, dtype=jnp.int32) // top_k
        row_token = jnp.full((n_rows,), tokens, jnp.int32).at[dest_row].set(pair_token, mode="drop")
        send_rows = jnp.take(hidden, row_token, axis=0, mode="fill", fill_value=0).reshape(per_dev, groups, capacity, hidden_dim)
        recv_rows = lax.all_to_all(send_rows, "ep", 1, 1, tiled=True)
        expert_out = expert_bank(recv_rows.reshape(per_dev, groups * capacity, hidden_dim), w_gate, w_up, w_down).astype(jnp.bfloat16)
        back_rows = lax.all_to_all(expert_out.reshape(per_dev, groups, capacity, hidden_dim), "ep", 1, 1, tiled=True)
        picked = jnp.take(back_rows.reshape(n_rows, hidden_dim), dest_row, axis=0, mode="fill", fill_value=0).reshape(tokens, top_k, hidden_dim)
        routed = jnp.sum(gate_vals[:, :, None] * picked.astype(jnp.float32), axis=1)
        shared = swiglu(hidden, shared_gate, shared_up, shared_down)
        return (shared + routed).astype(jnp.bfloat16)

    return jax.shard_map(device_fn, mesh=mesh, in_specs=(tok_spec, P(), bank_spec, bank_spec, bank_spec, P(), P(), P(), tok_spec, tok_spec), out_specs=tok_spec, check_vma=False)
```

profile of v0, /device:TPU:123, one launch (start us, length us, event | category | flops | bytes accessed | tf_op | source)
XLA Modules:
  0.0 2181.0 jit_solution(15165617184308836203)
XLA Ops:
  0.0 1.0 copy.70
  1.7 0.8 broadcast_compare_fusion
  2.8 0.4 gt.28
  3.2 0.4 gt.27
  4.0 0.4 gt.29
  4.6 18.8 reduce-window.6
  23.4 0.5 slice.14
  23.9 0.6 copy.85
  24.7 0.6 add_add_fusion
  25.3 0.7 fusion.1
  26.6 23.0 %scatter_custom_fusion = s32[12288]{0:T(1024)S(1)} fusion(s32[6144]{0:T(1024)S(1)} %bitcast.48, s32[6144]{0:T(1024)S(1)} %add_select_fusion.3, s32[]{:T(128)} %constant.101.clone.1), kind=kCustom, calls=%fused_computation.59 | custom fusion | bytes 49156 | tf_op jit(solution)/shard_map/scatter | solution.py:50
  49.8 94.1 %gather_fusion = bf16[12288,2048]{1,0:T(8,128)(2,1)} fusion(bf16[1024,2048]{1,0:T(8,128)(2,1)} %param.10, s32[12288]{0:T(1024)S(1)} %fusion.7), kind=kCustom, calls=%fused_computation | custom fusion | bytes 100712448 | tf_op jit(solution)/shard_map/jit(_take)/gather | solution.py:51
  143.9 33.8 %copy_select_fusion = bf16[2,32,192,2048]{3,2,0,1:T(8,128)(2,1)} fusion(bf16[2,32,192,2048]{3,2,1,0:T(8,128)(2,1)} %bitcast.40, pred[2,32,192]{2,0,1:T(4,128)(4,1)S(1)} %copy.80), kind=kLoop, calls=%fused_computation.6 | loop fusion | flops 25165824 | bytes 100675584 | tf_op jit(solution)/shard_map/jit(_take)/select_n | solution.py:51
  177.6 604.8 %all_to_all.10 = bf16[2,32,192,2048]{3,2,0,1:T(8,128)(2,1)} all-to-all(bf16[2,32,192,2048]{3,2,0,1:T(8,128)(2,1)} %copy_select_fusion), channel_id=1, replica_groups=mesh['dp'=1,'ep'=32] {'ep'}, dimensions={1} | all-to-all | bytes 100663296 | tf_op jit(solution)/shard_map/all_to_all | solution.py:52
  782.5 33.4 %copy.82 = bf16[2,32,192,2048]{3,2,1,0:T(8,128)(2,1)} copy(bf16[2,32,192,2048]{3,2,0,1:T(8,128)(2,1)} %all_to_all.10) | data formatting | bytes 100663296 | tf_op jit(solution)/shard_map/all_to_all | solution.py:52
  815.8 87.8 %fusion.27 = f32[2,6144,1408]{2,1,0:T(8,128)} fusion(bf16[2,6144,2048]{2,1,0:T(8,128)(2,1)} %bitcast.41, bf16[2,2048,1408]{2,1,0:T(8,128)(2,1)} %param.12), kind=kOutput, calls=%fused_computation.67 | convolution fusion | flops 70866960384 | bytes 131072000 | tf_op jit(solution)/shard_map/erd,edf->erf/dot_general | solution.py:17
  903.6 91.7 %multiply_convert_fusion = bf16[2,6144,1408]{2,1,0:T(8,128)(2,1)} fusion(f32[2,6144,1408]{2,1,0:T(8,128)} %fusion.27, bf16[2,6144,2048]{2,1,0:T(8,128)(2,1)} %bitcast.42, bf16[2,2048,1408]{2,1,0:T(8,128)(2,1)} %param.13), kind=kOutput, calls=%fused_computation.4 | convolution fusion | flops 70970769408 | bytes 165675008 | tf_op jit(solution)/shard_map/erd,edf->erf/dot_general | solution.py:18
  995.3 87.3 %convolution_convert_fusion = bf16[2,6144,2048]{2,1,0:T(8,128)(2,1)} fusion(bf16[2,6144,1408]{2,1,0:T(8,128)(2,1)} %multiply_convert_fusion, bf16[2,1408,2048]{2,1,0:T(8,128)(2,1)} %param.14), kind=kOutput, calls=%fused_computation.7 | convolution fusion | flops 70892126208 | bytes 96468992 | tf_op jit(solution)/shard_map/erf,efd->erd/dot_general | solution.py:20
  1082.6 33.4 %copy.83 = bf16[2,32,192,2048]{3,2,0,1:T(8,128)(2,1)} copy(bf16[2,32,192,2048]{3,2,1,0:T(8,128)(2,1)} %bitcast.43) | data formatting | bytes 100663296 | tf_op jit(solution)/shard_map/reshape | solution.py:54
  1116.1 59.7 %all-to-all-start.1 = ((bf16[2,32,192,2048]{3,2,0,1:T(8,128)(2,1)}), bf16[2,32,192,2048]{3,2,0,1:T(8,128)(2,1)}, u32[]{:S(2)}, u32[]{:S(2)}) async-start(bf16[2,32,192,2048]{3,2,0,1:T(8,128)(2,1)} %copy.83), calls=%async_computation.1 | async-start | bytes 100663296 | tf_op jit(solution)/shard_map/all_to_all | solution.py:54
  1175.7 0.5 reduce_sum.33
  1176.5 0.9 copy.77
  1178.0 3.6 fusion.25
  1181.7 49.3 %gather_fusion.2 = f32[6144]{0:T(1024)S(1)} fusion(f32[1024,64]{0,1:T(8,128)S(1)} %fusion.5, s32[6144]{0:T(1024)S(1)} %reshape.245), kind=kCustom, calls=%fused_computation.2 | custom fusion | bytes 98304 | tf_op jit(solution)/shard_map/jit(take_along_axis)/gather | solution.py:26
  1231.0 0.5 reshape.248
  1232.0 18.7 fusion.26
  1250.7 604.8 %all-to-all-done.1 = bf16[2,32,192,2048]{3,2,0,1:T(8,128)(2,1)} async-done(((bf16[2,32,192,2048]{3,2,0,1:T(8,128)(2,1)}), bf16[2,32,192,2048]{3,2,0,1:T(8,128)(2,1)}, u32[]{:S(2)}, u32[]{:S(2)}) %all-to-all-start.1) | async-done | bytes 50331680 | tf_op jit(solution)/shard_map/all_to_all | solution.py:54
  1855.5 33.4 %copy.84 = bf16[2,32,192,2048]{3,2,1,0:T(8,128)(2,1)} copy(bf16[2,32,192,2048]{3,2,0,1:T(8,128)(2,1)} %all-to-all-done.1) | data formatting | bytes 100663296 | tf_op jit(solution)/shard_map/all_to_all | solution.py:54
  1888.9 176.1 %gather_fusion.1 = bf16[6144,2048]{1,0:T(8,128)(2,1)} fusion(bf16[12288,2048]{1,0:T(8,128)(2,1)} %bitcast.39, s32[6144]{0:T(1024)S(1)} %broadcast_clamp_fusion), kind=kCustom, calls=%fused_computation.1 | custom fusion | bytes 50356224 | tf_op jit(solution)/shard_map/jit(_take)/gather | solution.py:55
  2065.0 39.5 %gather.20 = bf16[1024,6,2048]{2,1,0:T(8,128)(2,1)} reshape(bf16[6144,2048]{1,0:T(8,128)(2,1)} %gather_fusion.1) | data formatting | bytes 50331648 | tf_op jit(solution)/shard_map/jit(_take)/gather | solution.py:55
  2104.5 39.8 %multiply_reduce_fusion = f32[1024,2048]{1,0:T(8,128)} fusion(bf16[1024,6,2048]{2,1,0:T(8,128)(2,1)} %gather.20, f32[1024,6]{1,0:T(8,128)S(1)} %copy.69, pred[1024,6]{1,0:T(8,128)(4,1)S(1)} %copy-done.1), kind=kLoop, calls=%fused_computation.5 | loop fusion | flops 48234496 | bytes 33585152 | tf_op jit(solution)/shard_map/reduce_sum | solution.py:56
  2144.3 36.5 %add_convert_fusion = bf16[1024,2048]{1,0:T(8,128)(2,1)} fusion(f32[1024,2048]{1,0:T(8,128)} %multiply_reduce_fusion, bf16[2816,2048]{1,0:T(8,128)(2,1)} %param.17, f32[1024,2816]{1,0:T(8,128)} %fusion.26, bf16[1024,2048]{1,0:T(8,128)(2,1)} %param.10, bf16[2048,2816]{1,0:T(8,128)(2,1)} %param.16), kind=kOutput, calls=%fused_computation.9 | convolution fusion | flops 23643815936 | bytes 51380224 | tf_op jit(solution)/shard_map/dot_general | solution.py:13
  (43 shorter events, 3.9 us)
Async XLA Ops:
  0.0 1178.0 %copy-start = (bf16[2048,64]{0,1:T(8,128)(2,1)S(1)}, bf16[2048,64]{0,1:T(8,128)(2,1)}, u32[]{:S(2)}) copy-start(bf16[2048,64]{0,1:T(8,128)(2,1)} %param.11) | copy-start | bytes 786436
  26.0 0.6 copy-start.6
  26.6 117.3 %copy-start.8 = (s32[6144,1]{0,1:T(1,128)}, s32[6144,1]{0,1:T(1,128)S(1)}, u32[]{:S(2)}) copy-start(s32[6144,1]{0,1:T(1,128)S(1)} %compare_select_fusion) | copy-start | bytes 73732
  1116.0 59.7 %copy-start.7 = (s32[6144]{0:T(1024)S(1)}, s32[6144]{0:T(1024)}, u32[]{:S(2)}) copy-start(s32[6144]{0:T(1024)} %copy-done.6) | copy-start | bytes 73732
  1116.1 60.4 %copy-start.2 = (s32[1024,6]{0,1:T(8,128)S(1)}, s32[1024,6]{0,1:T(8,128)}, u32[]{:S(2)}) copy-start(s32[1024,6]{0,1:T(8,128)} %param.18) | copy-start | bytes 73732
  1116.1 60.4 %copy-start.4 = (s32[1024,6]{0,1:T(8,128)S(1)}, s32[1024,6]{0,1:T(8,128)}, u32[]{:S(2)}) copy-start(s32[1024,6]{0,1:T(8,128)} %param.19) | copy-start | bytes 73732
  1116.1 739.4 %all-to-all-start.1 = ((bf16[2,32,192,2048]{3,2,0,1:T(8,128)(2,1)}), bf16[2,32,192,2048]{3,2,0,1:T(8,128)(2,1)}, u32[]{:S(2)}, u32[]{:S(2)}) async-start(bf16[2,32,192,2048]{3,2,0,1:T(8,128)(2,1)} %copy.83), calls=%async_computation.1 | async-start | bytes 100663296 | tf_op jit(solution)/shard_map/all_to_all | solution.py:54
  1181.7 50.0 %copy-start.3 = (s32[1024,6]{0,1:T(8,128)S(1)}, s32[1024,6]{0,1:T(8,128)}, u32[]{:S(2)}) copy-start(s32[1024,6]{0,1:T(8,128)} %param.18) | copy-start | bytes 73732
  1181.7 50.0 %copy-start.5 = (s32[1024,6]{0,1:T(8,128)S(1)}, s32[1024,6]{0,1:T(8,128)}, u32[]{:S(2)}) copy-start(s32[1024,6]{0,1:T(8,128)} %param.19) | copy-start | bytes 73732
  1181.7 50.2 %copy-start.9 = (s32[6144,1]{0,1:T(1,128)S(1)}, s32[6144,1]{0,1:T(1,128)}, u32[]{:S(2)}) copy-start(s32[6144,1]{0,1:T(1,128)} %copy-done.8) | copy-start | bytes 73732
  2065.0 39.5 %copy-start.1 = (pred[1024,6]{1,0:T(8,128)(4,1)S(1)}, pred[1024,6]{1,0:T(8,128)(4,1)}, u32[]{:S(2)}) copy-start(pred[1024,6]{1,0:T(8,128)(4,1)} %copy.77) | copy-start | bytes 18436
where the time goes:
time: 2200 us; the launch traced here: 2180 us
  blocking collectives  605 us (28%)
  waiting for transfers between devices  605 us (28%)
  local copies, waits for them, and re-layouts  490 us (22%)
  matrix products  326 us (15%)
  other arithmetic  95.3 us (4%)
  starting transfers between devices  59.7 us (3%)
    all_to_all x1, blocking collectives, device_fn(): recv_rows = lax.all_to_all(send_rows, 'ep', 1, 1, tiled=True)  605 us
    all_to_all x1, waiting for transfers between devices, device_fn(): lax.all_to_all(expert_out.reshape(per_dev, groups, capacity, hidden_dim),...  605 us
    gather x2, local copies, waits for them, and re-layouts, device_fn(): jnp.take(back_rows.reshape(n_rows, hidden_dim), dest_row, axis=0, mode='f...  216 us
    gather x1, local copies, waits for them, and re-layouts, device_fn(): jnp.take(hidden, row_token, axis=0, mode='fill', fill_value=0)  94.1 us
    dot_general x1, matrix products, expert_bank(): jnp.einsum('erd,edf->erf', tok_rows, up_w, preferred_element_type=jnp.flo...  91.7 us
    dot_general x1, matrix products, expert_bank(): jnp.einsum('erd,edf->erf', tok_rows, gate_w, preferred_element_type=jnp.f...  87.8 us
    dot_general x1, matrix products, expert_bank(): jnp.einsum('erf,efd->erd', act_rows, down_w, preferred_element_type=jnp.f...  87.3 us
    all_to_all x1, starting transfers between devices, device_fn(): lax.all_to_all(expert_out.reshape(per_dev, groups, capacity, hidden_dim),...  59.7 us
  transfers between devices with their start and end apart: 1, of which 1 were waited for; matrix products, arithmetic and copies ran while one was open for 3% of the time, Pallas kernels for 0%

commit v1 on v0

v1 whole, which is shorter than its diff:
```python
import functools

import jax
import jax.numpy as jnp
from jax import lax
from jax.experimental import pallas as pl
from jax.experimental.pallas import tpu as pltpu
from jax.sharding import PartitionSpec as P

ROUTE_SCALE = 16.0
GROUP_BLOCKS = 4
COL = 256
VMEM_LIMIT = 63 * 1024 * 1024


def swiglu(tok_rows, gate_w, up_w, down_w):
    h_gate = jnp.dot(tok_rows, gate_w, preferred_element_type=jnp.float32)
    h_up = jnp.dot(tok_rows, up_w, preferred_element_type=jnp.float32)
    act_rows = (jax.nn.silu(h_gate) * h_up).astype(jnp.bfloat16)
    return jnp.dot(act_rows, down_w, preferred_element_type=jnp.float32)


def dot32(a, b):
    return jnp.dot(a, b, preferred_element_type=jnp.float32)


def expert_kernel(which, cap, tab_ref, x_ref, w1_ref, w3_ref, w2_ref, o_ref, rows, gates, act, tail):
    block = pl.program_id(0)
    slot = lax.rem(block, GROUP_BLOCKS)
    ff = w1_ref.shape[2]
    full = ff // COL * COL
    half = ff - full
    tokens = x_ref.shape[1]

    if half:
        @pl.when(block == 0)
        def _():
            tail[:, :half] = w1_ref[0, :, full:]
            tail[:, half:] = w3_ref[0, :, full:]

    per_dev = tab_ref.shape[1] // 2
    rank = tab_ref[0, which:which + 1, :].astype(jnp.int32)
    gate = tab_ref[0, per_dev + which:per_dev + which + 1, :]
    hit = rank == lax.broadcasted_iota(jnp.int32, (cap, tokens), 0)
    pick = jnp.where(hit, 1.0, 0.0).astype(jnp.bfloat16)
    at = pl.ds(pl.multiple_of(slot * cap, cap), cap)
    rows[at, :] = dot32(pick, x_ref[0]).astype(jnp.bfloat16)
    gates[at, :] = jnp.broadcast_to(jnp.sum(jnp.where(hit, gate, 0.0), axis=1, keepdims=True), (cap, 128))

    @pl.when(slot == GROUP_BLOCKS - 1)
    def _():
        tok = rows[...]
        for c in range(0, full, COL):
            h_gate = dot32(tok, w1_ref[0, :, c:c + COL])
            h_up = dot32(tok, w3_ref[0, :, c:c + COL])
            act[:, c:c + COL] = (jax.nn.silu(h_gate) * h_up).astype(jnp.bfloat16)
        if half:
            h_both = dot32(tok, tail[...])
            act[:, full:] = (jax.nn.silu(h_both[:, :half]) * h_both[:, half:]).astype(jnp.bfloat16)
        a = act[...]
        g = gates[:, :1]
        for c in range(0, w2_ref.shape[2], COL):
            e = dot32(a, w2_ref[0, :, c:c + COL]).astype(jnp.bfloat16).astype(jnp.float32)
            o_ref[:, :, c:c + COL] = (g * e).astype(jnp.bfloat16).reshape(GROUP_BLOCKS, cap, COL)


def expert_call(which, cap, tab, x_all, w1, w3, w2):
    blocks, tokens, dim = x_all.shape
    ff = w1.shape[2]
    once = pl.Buffered(1)
    rows = GROUP_BLOCKS * cap
    return pl.pallas_call(
        functools.partial(expert_kernel, which, cap),
        grid=(blocks,),
        in_specs=[
            pl.BlockSpec((1,) + tab.shape[1:], lambda b: (b, 0, 0)),
            pl.BlockSpec((1, tokens, dim), lambda b: (b, 0, 0)),
            pl.BlockSpec((1, dim, ff), lambda b: (which, 0, 0), pipeline_mode=once),
            pl.BlockSpec((1, dim, ff), lambda b: (which, 0, 0), pipeline_mode=once),
            pl.BlockSpec((1, ff, dim), lambda b: (which, 0, 0), pipeline_mode=once),
        ],
        out_specs=pl.BlockSpec((GROUP_BLOCKS, cap, dim), lambda b: (b // GROUP_BLOCKS, 0, 0)),
        out_shape=jax.ShapeDtypeStruct((blocks, cap, dim), jnp.bfloat16),
        scratch_shapes=[
            pltpu.VMEM((rows, dim), jnp.bfloat16),
            pltpu.VMEM((rows, 128), jnp.float32),
            pltpu.VMEM((rows, ff), jnp.bfloat16),
            pltpu.VMEM((dim, COL), jnp.bfloat16),
        ],
        compiler_params=pltpu.CompilerParams(dimension_semantics=("arbitrary",), vmem_limit_bytes=VMEM_LIMIT),
        cost_estimate=pl.CostEstimate(
            flops=2 * blocks * cap * dim * (3 * ff + tokens), bytes_accessed=2 * x_all.size, transcendentals=0),
        name=f"expert{which}",
    )(tab, x_all, w1, w3, w2)


def combine_kernel(cap, r_ref, back_ref, y_ref, o_ref, acc):
    step = pl.program_id(0)
    tokens, per = r_ref.shape[1], r_ref.shape[2]

    @pl.when(step == 0)
    def _():
        acc[...] = y_ref[...]

    ranks = r_ref[0]
    lanes = lax.broadcasted_iota(jnp.int32, (tokens, 128), 1)
    tiles = []
    for lo in range(0, per * cap, 128):
        hit = None
        for w in range(lo // cap, (lo + 127) // cap + 1):
            col = ranks[:, w:w + 1]
            now = jnp.where(col >= 0, col + (w * cap - lo), -1) == lanes
            hit = now if hit is None else hit | now
        tiles.append(jnp.where(hit, 1.0, 0.0).astype(jnp.bfloat16))
    pick = jnp.concatenate(tiles, axis=1)
    for c in range(0, acc.shape[1], 512):
        acc[:, c:c + 512] += dot32(pick, back_ref[0, :, c:c + 512])

    @pl.when(step == pl.num_programs(0) - 1)
    def _():
        o_ref[...] = acc[...].astype(o_ref.dtype)


def combine_call(cap, ranks, back, y, out_dtype):
    steps, tokens, per = ranks.shape
    dim = y.shape[1]
    return pl.pallas_call(
        functools.partial(combine_kernel, cap),
        grid=(steps,),
        in_specs=[
            pl.BlockSpec((1, tokens, per), lambda i: (i, 0, 0)),
            pl.BlockSpec((1, per * cap, dim), lambda i: (i, 0, 0)),
            pl.BlockSpec((tokens, dim), lambda i: (0, 0), pipeline_mode=pl.Buffered(1)),
        ],
        out_specs=pl.BlockSpec((tokens, dim), lambda i: (0, 0), pipeline_mode=pl.Buffered(1)),
        out_shape=jax.ShapeDtypeStruct((tokens, dim), out_dtype),
        scratch_shapes=[pltpu.VMEM((tokens, dim), jnp.float32)],
        compiler_params=pltpu.CompilerParams(dimension_semantics=("arbitrary",), vmem_limit_bytes=VMEM_LIMIT),
        cost_estimate=pl.CostEstimate(flops=2 * tokens * back.size, bytes_accessed=2 * back.size, transcendentals=0),
        name="combine",
    )(ranks, back.reshape(steps, per * cap, dim), y)


def routing(hidden, w_router, top_idx, keep_mask):
    experts = w_router.shape[1]
    tokens = hidden.shape[0]
    logits = jnp.dot(hidden, w_router, preferred_element_type=jnp.float32)
    prob = jax.nn.softmax(logits, axis=-1)
    chosen = (top_idx[:, :, None] == jnp.arange(experts)[None, None, :]) & (keep_mask[:, :, None] > 0)
    member = jnp.any(chosen, axis=1)
    lower = (jnp.arange(tokens)[:, None] >= jnp.arange(tokens)[None, :]).astype(jnp.bfloat16)
    count = jnp.dot(lower, member.astype(jnp.bfloat16), preferred_element_type=jnp.float32)
    rank = jnp.where(member, count - 1.0, -1.0)
    gate = jnp.where(member, ROUTE_SCALE * prob, 0.0)
    return rank, gate


def solution(mesh):
    groups = mesh.shape["ep"]
    tok_spec = P(("dp", "ep"), None)
    bank_spec = P("ep", None, None)

    def device_fn(hidden, w_router, w_gate, w_up, w_down, shared_gate, shared_up, shared_down, top_idx, keep_mask):
        tokens, top_k = top_idx.shape
        dim = hidden.shape[1]
        experts = w_router.shape[1]
        per_dev = w_gate.shape[0]
        cap = 8 * ((top_k * tokens + 4 * experts - 1) // (4 * experts))
        x_all = lax.all_gather(hidden, "ep", axis=0, tiled=True).reshape(groups, tokens, dim)
        rank, gate = routing(hidden, w_router, top_idx, keep_mask)
        table = jnp.concatenate([rank.T.reshape(groups, per_dev, tokens), gate.T.reshape(groups, per_dev, tokens)], axis=1)
        table = lax.all_to_all(table, "ep", 0, 0, tiled=True)
        y = swiglu(hidden, shared_gate, shared_up, shared_down)
        backs = []
        for which in range(per_dev):
            out = expert_call(which, cap, table, x_all, w_gate, w_up, w_down)
            backs.append(lax.all_to_all(out, "ep", 0, 0, tiled=True))
        per = 4
        for which in range(per_dev):
            ranks = rank[:, which::per_dev].astype(jnp.int32).reshape(tokens, groups // per, per).transpose(1, 0, 2)
            last = which == per_dev - 1
            y = combine_call(cap, ranks, backs[which], y, jnp.bfloat16 if last else jnp.float32)
        return y

    return jax.shard_map(device_fn, mesh=mesh, in_specs=(tok_spec, P(), bank_spec, bank_spec, bank_spec, P(), P(), P(), tok_spec, tok_spec), out_specs=tok_spec, check_vma=False)
```

time: 2200 us -> 1310 us (0.60)
  the two profiles are of different devices: /device:TPU:123 before, /device:TPU:107 now
where the time goes in v1:
time: 1310 us
  waiting for transfers between devices  727 us (55%)
  Pallas kernels  469 us (36%)
  matrix products  59.1 us (5%)
  blocking collectives  21 us (2%)
  between operations  13.7 us (1%)
    pallas_call x2, Pallas kernels, expert_call(): pl.pallas_call(functools.partial(expert_kernel, which, cap), grid=(blocks...  384 us
    all_to_all x2, waiting for transfers between devices, device_fn(): backs.append(lax.all_to_all(out, 'ep', 0, 0, tiled=True))  379 us
    all_gather x1, waiting for transfers between devices, device_fn(): lax.all_gather(hidden, 'ep', axis=0, tiled=True)  347 us
    pallas_call x2, Pallas kernels, combine_call(): pl.pallas_call(functools.partial(combine_kernel, cap), grid=(steps,), in_...  85.1 us
    dot_general x1, matrix products, swiglu(): return jnp.dot(act_rows, down_w, preferred_element_type=jnp.float32)  36.2 us
  transfers between devices with their start and end apart: 3, of which 3 were waited for; matrix products, arithmetic and copies ran while one was open for 5% of the time, Pallas kernels for 18%

profile of v1, /device:TPU:107, one launch (start us, length us, event | category | flops | bytes accessed | tf_op | source)
XLA Modules:
  0.0 1310.5 jit_solution(1528238549534968924)
XLA Ops:
  6.5 0.0 copy-start
  6.6 0.0 all-gather.2.cloned.1.call-start
  6.6 0.7 all-gather.2.cloned.1.call-update
  7.3 0.2 copy-done
  7.5 3.6 fusion.6
  11.1 0.1 fusion.5
  11.2 0.8 broadcast_compare_fusion
  11.9 1.0 fusion.2
  12.9 0.1 select_bitcast_fusion
  13.0 0.1 reshape.28
  13.2 0.6 fusion.4
  13.8 0.0 copy-start.2
  13.8 0.1 reshape.27
  13.9 0.2 pad_maximum_fusion
  14.2 21.0 %all_to_all.15.tab_ref = f32[32,4,1024]{2,1,0:T(4,128)} all-to-all(f32[32,4,1024]{2,1,0:T(4,128)S(1)} %pad_maximum_fusion), channel_id=1, replica_groups=mesh['dp'=1,'ep'=32] {'ep'}, dimensions={0} | all-to-all | bytes 1048576 | tf_op jit(solution)/shard_map/all_to_all | solution.py:172
  35.2 347.1 %all-gather.2.cloned.1.call-done = bf16[32768,2048]{1,0:T(8,128)(2,1)} async-done(((bf16[1024,2048]{1,0:T(8,128)(2,1)}), bf16[32768,2048]{1,0:T(8,128)(2,1)}) %all-gather.2.cloned.1.call-update) | async-done | bytes 134217744 | tf_op jit(solution)/shard_map/all_gather | solution.py:169
  382.4 192.1 %expert0.1 = bf16[32,192,2048]{2,1,0:T(8,128)(2,1)} custom-call(f32[32,4,1024]{2,1,0:T(4,128)} %all_to_all.15.tab_ref, bf16[32,1024,2048]{2,1,0:T(8,128)(2,1)} %bitcast.3.x_ref, bf16[2,2048,1408]{2,1,0:T(8,128)(2,1)} %w1_ref.3, bf16[2,2048,1408]{2,1,0:T(8,128)(2,1)} %w3_ref.3, bf16[2,1408,2048]{2,1,0:T(8,128)(2,1)} %w2_ref.3), custom_call_target="tpu_custom_call" | custom-call | flops 132070244352 | bytes 134217728 | tf_op jit(solution)/shard_map/expert0/pallas_call | solution.py:72
  574.4 0.0 copy-done.2
  574.5 7.4 all-to-all-start.2
  581.8 192.2 %expert1.1 = bf16[32,192,2048]{2,1,0:T(8,128)(2,1)} custom-call(f32[32,4,1024]{2,1,0:T(4,128)} %all_to_all.15.tab_ref, bf16[32,1024,2048]{2,1,0:T(8,128)(2,1)} %bitcast.3.x_ref, bf16[2,2048,1408]{2,1,0:T(8,128)(2,1)} %w1_ref.3, bf16[2,2048,1408]{2,1,0:T(8,128)(2,1)} %w3_ref.3, bf16[2,1408,2048]{2,1,0:T(8,128)(2,1)} %w2_ref.3), custom_call_target="tpu_custom_call" | custom-call | flops 132070244352 | bytes 134217728 | tf_op jit(solution)/shard_map/expert1/pallas_call | solution.py:72
  774.0 0.0 copy-start.3
  774.0 145.9 %all-to-all-done.2 = bf16[32,192,2048]{2,1,0:T(8,128)(2,1)} async-done(((bf16[32,192,2048]{2,1,0:T(8,128)(2,1)}), bf16[32,192,2048]{2,1,0:T(8,128)(2,1)}, u32[]{:S(2)}, u32[]{:S(2)}) %all-to-all-start.2) | async-done | bytes 25165856 | tf_op jit(solution)/shard_map/all_to_all | solution.py:177
  919.9 4.8 all-to-all-start.1
  924.6 0.0 copy-done.3
  924.8 2.7 copy.18
  927.6 2.7 copy.17
  930.2 18.8 %fusion.7 = f32[1024,2816]{1,0:T(8,128)} fusion(bf16[1024,2048]{1,0:T(8,128)(2,1)} %param.10, bf16[2048,2816]{1,0:T(8,128)(2,1)} %param.15), kind=kOutput, calls=%fused_computation.14 | convolution fusion | flops 11811160064 | bytes 27262976 | tf_op jit(solution)/shard_map/dot_general | solution.py:17
  949.0 36.2 %fusion.8.y_ref = f32[1024,2048]{1,0:T(8,128)} fusion(bf16[2816,2048]{1,0:T(8,128)(2,1)} %param.17, f32[1024,2816]{1,0:T(8,128)} %fusion.7, bf16[1024,2048]{1,0:T(8,128)(2,1)} %param.10, bf16[2048,2816]{1,0:T(8,128)(2,1)} %param.16), kind=kOutput, calls=%fused_computation.15 | convolution fusion | flops 23639621632 | bytes 47185920 | tf_op jit(solution)/shard_map/dot_general | solution.py:20
  985.2 43.3 %combine.2.y_ref = f32[1024,2048]{1,0:T(8,128)} custom-call(s32[8,1024,4]{2,1,0:T(8,128)} %bitcast.30, bf16[8,768,2048]{2,1,0:T(8,128)(2,1)} %bitcast.6.back_ref, f32[1024,2048]{1,0:T(8,128)} %fusion.8.y_ref), custom_call_target="tpu_custom_call" | custom-call | flops 25769803776 | bytes 25165824 | tf_op jit(solution)/shard_map/combine/pallas_call | solution.py:127
  1028.5 233.1 %all-to-all-done.1 = bf16[32,192,2048]{2,1,0:T(8,128)(2,1)} async-done(((bf16[32,192,2048]{2,1,0:T(8,128)(2,1)}), bf16[32,192,2048]{2,1,0:T(8,128)(2,1)}, u32[]{:S(2)}, u32[]{:S(2)}) %all-to-all-start.1) | async-done | bytes 25165856 | tf_op jit(solution)/shard_map/all_to_all | solution.py:177
  1261.7 41.8 %combine.3 = bf16[1024,2048]{1,0:T(8,128)(2,1)} custom-call(s32[8,1024,4]{2,1,0:T(8,128)} %bitcast.29, bf16[8,768,2048]{2,1,0:T(8,128)(2,1)} %bitcast.4.back_ref, f32[1024,2048]{1,0:T(8,128)} %combine.2.y_ref), custom_call_target="tpu_custom_call" | custom-call | flops 25769803776 | bytes 25165824 | tf_op jit(solution)/shard_map/combine/pallas_call | solution.py:127
  1303.5 0.0 copy-done.1
  (7 shorter events, 0.2 us)
Async XLA Ops:
  6.5 1.0 copy-start
  6.6 375.8 %all-gather.2.cloned.1.call-start = ((), (), s32[]{:S(2)}) async-start(), calls=%async_computation.3 | async-start | bytes 138412032 | tf_op jit(solution)/shard_map/all_gather | solution.py:169
  13.8 560.7 %copy-start.2 = (f32[1024,64]{0,1:T(8,128)}, f32[1024,64]{0,1:T(8,128)S(1)}, u32[]{:S(2)}) copy-start(f32[1024,64]{0,1:T(8,128)S(1)} %fusion.4) | copy-start | bytes 786436
  574.5 345.4 %all-to-all-start.2 = ((bf16[32,192,2048]{2,1,0:T(8,128)(2,1)}), bf16[32,192,2048]{2,1,0:T(8,128)(2,1)}, u32[]{:S(2)}, u32[]{:S(2)}) async-start(bf16[32,192,2048]{2,1,0:T(8,128)(2,1)} %expert0.1), calls=%async_computation.2 | async-start | bytes 50331648 | tf_op jit(solution)/shard_map/all_to_all | solution.py:177
  774.0 150.7 %copy-start.3 = (f32[1024,64]{0,1:T(8,128)S(1)}, f32[1024,64]{0,1:T(8,128)}, u32[]{:S(2)}) copy-start(f32[1024,64]{0,1:T(8,128)} %copy-done.2) | copy-start | bytes 786436
  919.9 341.8 %all-to-all-start.1 = ((bf16[32,192,2048]{2,1,0:T(8,128)(2,1)}), bf16[32,192,2048]{2,1,0:T(8,128)(2,1)}, u32[]{:S(2)}, u32[]{:S(2)}) async-start(bf16[32,192,2048]{2,1,0:T(8,128)(2,1)} %expert1.1), calls=%async_computation.1 | async-start | bytes 50331648 | tf_op jit(solution)/shard_map/all_to_all | solution.py:177
  1261.7 41.8 %copy-start.1 = (bf16[2048,64]{0,1:T(8,128)(2,1)S(1)}, bf16[2048,64]{0,1:T(8,128)(2,1)}, u32[]{:S(2)}) copy-start(bf16[2048,64]{0,1:T(8,128)(2,1)} %param.11) | copy-start | bytes 786436
Sparse Core Ops, SparseCore 0:
  9.4 372.8 all-gather.1

commit v2 on v0

v2 whole, which is shorter than its diff:
```python
import functools
import math

import jax
import jax.numpy as jnp
from jax import lax
from jax.experimental import pallas as pl
from jax.experimental.pallas import tpu as pltpu
from jax.sharding import PartitionSpec as P

ROUTE_SCALE = 16.0
CORES = 2
COL = 256
VMEM_LIMIT = 63 * 1024 * 1024
MESH = pl.DeviceIdType.MESH


def swiglu(tok_rows, gate_w, up_w, down_w):
    h_gate = jnp.dot(tok_rows, gate_w, preferred_element_type=jnp.float32)
    h_up = jnp.dot(tok_rows, up_w, preferred_element_type=jnp.float32)
    act_rows = (jax.nn.silu(h_gate) * h_up).astype(jnp.bfloat16)
    return jnp.dot(act_rows, down_w, preferred_element_type=jnp.float32)


def dot32(a, b):
    return jnp.dot(a, b, preferred_element_type=jnp.float32)


def place(side):
    me = lax.axis_index("ep")
    return lax.rem(me // CORES, side), me // (CORES * side), lax.rem(me, CORES)


def device(side, x, y, k):
    return (lax.rem(y, side) * side + lax.rem(x, side)) * CORES + lax.rem(k, CORES)


def expert_kernel(side, cap, tab_ref, x_ref, w1_ref, w3_ref, w2_ref, recv, stage, xbuf, rows, act, tail, tile,
                  x_sem, stage_sem, send_a, recv_a, send_b, recv_b, self_sem):
    which, turn = pl.program_id(0), pl.program_id(1)
    turns = pl.num_programs(1)
    step = which * turns + turn
    steps = pl.num_programs(0) * turns
    ff = w1_ref.shape[2]
    full = ff // COL * COL
    rest = ff - full
    tokens, dim = x_ref.shape[1], x_ref.shape[2]
    half = dim // 2
    x, y, k = place(side)

    def offsets(s):
        i = lax.rem(s, turns)
        return s // turns, lax.rem(i // CORES + 1, side), lax.rem(i + 1, CORES)

    def fetch(s, j):
        _, dy, dc = offsets(s)
        return pltpu.make_async_copy(x_ref.at[device(side, x + j, y + dy, k + dc)], xbuf.at[j], x_sem.at[j])

    def to_column(s):
        e, dy, dc = offsets(s)
        return pltpu.make_async_remote_copy(
            src_ref=stage.at[s, 0], dst_ref=recv.at[0, y * CORES + k, e], send_sem=send_a.at[s], recv_sem=recv_a.at[s],
            device_id={"ep": device(side, x, y + dy, k + dc)}, device_id_type=MESH)

    def to_row(s, dx):
        e, dy, dc = offsets(s)
        return pltpu.make_async_remote_copy(
            src_ref=stage.at[s, 1, dx], dst_ref=recv.at[1, x * CORES + k, e, dy], send_sem=send_b.at[s, dx], recv_sem=recv_b.at[s, dx],
            device_id={"ep": device(side, x + dx, y, k + dc)}, device_id_type=MESH)

    def keep_column(s):
        e, _, _ = offsets(s)
        return pltpu.make_async_copy(tile.at[0], recv.at[0, y * CORES + k, e], self_sem.at[0])

    def keep_row(s):
        e, dy, _ = offsets(s)
        return pltpu.make_async_copy(tile.at[1, 0], recv.at[1, x * CORES + k, e, dy], self_sem.at[1])

    def put(s):
        return pltpu.make_async_copy(tile, stage.at[s], stage_sem)

    def remotes(s, act_on):
        _, dy, dc = offsets(s)

        @pl.when((dy != 0) | (dc != 0))
        def _():
            act_on(to_column(s))

        @pl.when(dc != 0)
        def _():
            act_on(to_row(s, 0))

        for dx in range(1, side):
            act_on(to_row(s, dx))

    def locals_(s, act_on):
        _, dy, dc = offsets(s)

        @pl.when((dy == 0) & (dc == 0))
        def _():
            act_on(keep_column(s))

        @pl.when(dc == 0)
        def _():
            act_on(keep_row(s))

    def flush(s):
        put(s).wait()
        locals_(s, lambda c: c.wait())
        remotes(s, lambda c: c.start())

    @pl.when(step == 0)
    def _():
        for j in range(side):
            fetch(0, j).start()

    if rest:
        @pl.when(turn == 0)
        def _():
            tail[:, :rest] = w1_ref[0, :, full:]
            tail[:, rest:] = w3_ref[0, :, full:]

    _, now_y, now_c = offsets(step)

    @pl.loop(0, side)
    def _(j):
        fetch(step, j).wait()
        rank = tab_ref[device(side, x + j, y + now_y, k + now_c), pl.ds(which, 1), :]
        hit = rank == lax.broadcasted_iota(jnp.int32, (cap, tokens), 0).astype(jnp.float32)
        pick = jnp.where(hit, 1.0, 0.0).astype(jnp.bfloat16)
        rows[pl.ds(pl.multiple_of(j * cap, cap), cap), :] = dot32(pick, xbuf[j]).astype(jnp.bfloat16)

        @pl.when(step + 1 < steps)
        def _():
            fetch(step + 1, j).start()

    @pl.when(step > 0)
    def _():
        flush(step - 1)

    tok = rows[...]
    for c in range(0, full, COL):
        h_gate = dot32(tok, w1_ref[0, :, c:c + COL])
        h_up = dot32(tok, w3_ref[0, :, c:c + COL])
        act[:, c:c + COL] = (jax.nn.silu(h_gate) * h_up).astype(jnp.bfloat16)
    if rest:
        h_both = dot32(tok, tail[...])
        act[:, full:] = (jax.nn.silu(h_both[:, :rest]) * h_both[:, rest:]).astype(jnp.bfloat16)
    a = act[...]
    for c in range(0, dim, COL):
        e = dot32(a, w2_ref[0, :, c:c + COL]).astype(jnp.bfloat16)
        at = c % half
        tile[c // half, :, :, at:at + COL] = e.reshape(side, cap, COL)

    put(step).start()
    locals_(step, lambda c: c.start())

    @pl.when(step == steps - 1)
    def _():
        flush(step)

        @pl.loop(0, steps)
        def _(s):
            remotes(s, lambda c: c.wait())


def expert_call(side, cap, tab, x_all, w1, w3, w2):
    blocks, tokens, dim = x_all.shape
    experts, _, ff = w1.shape
    once = pl.Buffered(1)
    turns = side * CORES
    steps = experts * turns
    rows = side * cap
    dma = pltpu.SemaphoreType.DMA
    recv, _ = pl.pallas_call(
        functools.partial(expert_kernel, side, cap),
        grid=(experts, turns),
        in_specs=[
            pl.BlockSpec(tab.shape, lambda e, t: (0, 0, 0), pipeline_mode=once),
            pl.BlockSpec(memory_space=pl.ANY),
            pl.BlockSpec((1, dim, ff), lambda e, t: (e, 0, 0), pipeline_mode=once),
            pl.BlockSpec((1, dim, ff), lambda e, t: (e, 0, 0), pipeline_mode=once),
            pl.BlockSpec((1, ff, dim), lambda e, t: (e, 0, 0), pipeline_mode=once),
        ],
        out_specs=[pl.BlockSpec(memory_space=pl.ANY)] * 2,
        out_shape=[
            jax.ShapeDtypeStruct((2, turns, experts, side, cap, dim // 2), jnp.bfloat16),
            jax.ShapeDtypeStruct((steps, 2, side, cap, dim // 2), jnp.bfloat16),
        ],
        scratch_shapes=[
            pltpu.VMEM((side, tokens, dim), jnp.bfloat16),
            pltpu.VMEM((rows, dim), jnp.bfloat16),
            pltpu.VMEM((rows, ff), jnp.bfloat16),
            pltpu.VMEM((dim, COL), jnp.bfloat16),
            pltpu.VMEM((2, side, cap, dim // 2), jnp.bfloat16),
            dma((side,)), dma, dma((steps,)), dma((steps,)), dma((steps, side)), dma((steps, side)), dma((2,)),
        ],
        compiler_params=pltpu.CompilerParams(
            dimension_semantics=("arbitrary", "arbitrary"), vmem_limit_bytes=VMEM_LIMIT, has_side_effects=True),
        cost_estimate=pl.CostEstimate(
            flops=2 * experts * blocks * cap * dim * (3 * ff + tokens), bytes_accessed=4 * x_all.size, transcendentals=0),
        name="experts",
    )(tab, x_all, w1, w3, w2)
    return recv


def combine_kernel(side, cap, t_ref, in_ref, recv, stage, pick, gate, acc, tile, stage_sem, send_sem, recv_sem, self_sem):
    turn, part = pl.program_id(0), pl.program_id(1)
    step = turn * 2 + part
    steps = 2 * side
    tokens = t_ref.shape[2]
    count = t_ref.shape[3] // 2
    experts = in_ref.shape[2]
    half = in_ref.shape[5]
    x, y, k = place(side)

    def offsets(s):
        return lax.rem(s // 2 + 1, side), lax.rem(s, 2)

    def send(s):
        rel, h = offsets(s)
        return pltpu.make_async_remote_copy(
            src_ref=stage.at[s], dst_ref=recv.at[h, rel], send_sem=send_sem.at[s], recv_sem=recv_sem.at[s],
            device_id={"ep": device(side, x + rel * (1 - h), y + rel * h, k)}, device_id_type=MESH)

    def put(s):
        return pltpu.make_async_copy(tile, stage.at[s], stage_sem)

    def keep(s):
        rel, h = offsets(s)
        return pltpu.make_async_copy(tile, recv.at[h, rel], self_sem)

    away = steps - 2

    @pl.when((step > 0) & (step <= away))
    def _():
        put(step - 1).wait()
        send(step - 1).start()

    @pl.when(step > away)
    def _():
        keep(step - 1).wait()

    lanes = lax.broadcasted_iota(jnp.int32, (tokens, cap), 1).astype(jnp.float32)
    for e in range(count):
        pick[e] = jnp.where(t_ref[0, 0, :, e:e + 1] == lanes, 1.0, 0.0).astype(jnp.bfloat16)
        gate[e] = jnp.broadcast_to(t_ref[0, 0, :, count + e:count + e + 1], (tokens, 128))

    acc[...] = jnp.zeros_like(acc)

    @pl.loop(0, count // 2)
    def _(pair):
        for c in range(0, half, COL):
            total = None
            for e in (2 * pair, 2 * pair + 1):
                wide = jnp.concatenate([gate[e]] * (COL // 128), axis=1)
                term = wide * dot32(pick[e], in_ref[0, e // experts, lax.rem(e, experts), 0, :, c:c + COL])
                total = term if total is None else total + term
            acc[:, c:c + COL] += total

    tile[...] = acc[...].astype(jnp.bfloat16)

    @pl.when(step < away)
    def _():
        put(step).start()

    @pl.when(step >= away)
    def _():
        keep(step).start()

    @pl.when(step == steps - 1)
    def _():
        keep(step).wait()

        @pl.loop(0, away)
        def _(s):
            send(s).wait()


def combine_call(side, cap, table, rows):
    _, _, tokens, width = table.shape
    turns, experts, half = rows.shape[1], rows.shape[2], rows.shape[5]
    count = width // 2
    dma = pltpu.SemaphoreType.DMA
    recv, _ = pl.pallas_call(
        functools.partial(combine_kernel, side, cap),
        grid=(side, 2),
        in_specs=[
            pl.BlockSpec((1, 1, tokens, width), lambda r, h: (h, (r + 1) % side, 0, 0)),
            pl.BlockSpec((1, turns, experts, 1, cap, half), lambda r, h: (h, 0, 0, (r + 1) % side, 0, 0)),
        ],
        out_specs=[pl.BlockSpec(memory_space=pl.ANY)] * 2,
        out_shape=[
            jax.ShapeDtypeStruct((2, side, tokens, half), jnp.bfloat16),
            jax.ShapeDtypeStruct((2 * side, tokens, half), jnp.bfloat16),
        ],
        scratch_shapes=[
            pltpu.VMEM((count, tokens, cap), jnp.bfloat16),
            pltpu.VMEM((count, tokens, 128), jnp.float32),
            pltpu.VMEM((tokens, half), jnp.float32),
            pltpu.VMEM((tokens, half), jnp.bfloat16),
            dma, dma((2 * side,)), dma((2 * side,)), dma,
        ],
        compiler_params=pltpu.CompilerParams(
            dimension_semantics=("arbitrary", "arbitrary"), vmem_limit_bytes=VMEM_LIMIT, has_side_effects=True),
        cost_estimate=pl.CostEstimate(flops=2 * tokens * rows.size, bytes_accessed=2 * rows.size, transcendentals=0),
        name="combine",
    )(table, rows)
    return recv


def routing(hidden, w_router, top_idx, keep_mask):
    experts = w_router.shape[1]
    tokens = hidden.shape[0]
    logits = jnp.dot(hidden, w_router, preferred_element_type=jnp.float32)
    prob = jax.nn.softmax(logits, axis=-1)
    chosen = (top_idx[:, :, None] == jnp.arange(experts)[None, None, :]) & (keep_mask[:, :, None] > 0)
    member = jnp.any(chosen, axis=1)
    lower = (jnp.arange(tokens)[:, None] >= jnp.arange(tokens)[None, :]).astype(jnp.bfloat16)
    count = jnp.dot(lower, member.astype(jnp.bfloat16), preferred_element_type=jnp.float32)
    rank = jnp.where(member, count - 1.0, -1.0)
    gate = jnp.where(member, ROUTE_SCALE * prob, 0.0)
    return rank, gate


def solution(mesh):
    groups = mesh.shape["ep"]
    side = math.isqrt(groups // CORES)
    tok_spec = P(("dp", "ep"), None)
    bank_spec = P("ep", None, None)
    rows_of = [[(y * side + x) * CORES + k for x in range(side)] for y in range(side) for k in range(CORES)]
    cols_of = [[(y * side + x) * CORES + k for y in range(side)] for x in range(side) for k in range(CORES)]

    def device_fn(hidden, w_router, w_gate, w_up, w_down, shared_gate, shared_up, shared_down, top_idx, keep_mask):
        tokens, top_k = top_idx.shape
        dim = hidden.shape[1]
        experts = w_router.shape[1]
        per_dev = w_gate.shape[0]
        cap = 8 * ((top_k * tokens + 4 * experts - 1) // (4 * experts))
        x_all = lax.all_gather(hidden, "ep", axis=0, tiled=True).reshape(groups, tokens, dim)
        rank, gate = routing(hidden, w_router, top_idx, keep_mask)
        table = lax.all_to_all(rank.T.reshape(groups, per_dev, tokens), "ep", 0, 0, tiled=True)
        here_x, here_y, _ = place(side)
        both = jnp.stack([rank, gate], axis=1).reshape(tokens, 2, side, side, CORES * per_dev)

        def exchange(blocks, peers, at):
            flat = blocks.reshape(side, tokens, 2 * side * CORES * per_dev)
            got = lax.all_to_all(flat, "ep", 0, 0, tiled=True, axis_index_groups=peers)
            return lax.dynamic_slice_in_dim(jnp.concatenate([got, got], axis=0), at, side, axis=0)

        by_x = exchange(both.transpose(3, 0, 1, 2, 4), rows_of, here_x)
        by_y = exchange(both.transpose(2, 0, 1, 3, 4), cols_of, here_y)
        pairs = jnp.stack([by_x, by_y])
        y = swiglu(hidden, shared_gate, shared_up, shared_down)
        x_all, y, pairs = lax.optimization_barrier((x_all, y, pairs))
        expert_rows = expert_call(side, cap, table, x_all, w_gate, w_up, w_down)
        sums = combine_call(side, cap, pairs, expert_rows).astype(jnp.float32)
        routed = jnp.concatenate([jnp.sum(sums[0], axis=0), jnp.sum(sums[1], axis=0)], axis=1)
        return (y + routed).astype(jnp.bfloat16)

    return jax.shard_map(device_fn, mesh=mesh, in_specs=(tok_spec, P(), bank_spec, bank_spec, bank_spec, P(), P(), P(), tok_spec, tok_spec), out_specs=tok_spec, check_vma=False)
```

time: 2200 us -> 989 us (0.45)
  the two profiles are of different devices: /device:TPU:123 before, /device:TPU:97 now
where the time goes in v2:
time: 989 us; the launch traced here: 983 us
  Pallas kernels  545 us (55%)
  waiting for transfers between devices  302 us (31%)
  matrix products  59.2 us (6%)
  other arithmetic  36.9 us (4%)
  starting transfers between devices  19 us (2%)
  between operations  14 us (1%)
    pallas_call x1, Pallas kernels, expert_call(): pl.pallas_call(functools.partial(expert_kernel, side, cap), grid=(experts...  379 us
    all_gather x1, waiting for transfers between devices, device_fn(): lax.all_gather(hidden, 'ep', axis=0, tiled=True)  301 us
    pallas_call x1, Pallas kernels, combine_call(): pl.pallas_call(functools.partial(combine_kernel, side, cap), grid=(side,...  167 us
    dot_general x1, matrix products, swiglu(): return jnp.dot(act_rows, down_w, preferred_element_type=jnp.float32)  36.3 us
  transfers between devices with their start and end apart: 4, of which 1 were waited for; matrix products, arithmetic and copies ran while one was open for 7% of the time, Pallas kernels for 0%

profile of v2, /device:TPU:97, one launch (start us, length us, event | category | flops | bytes accessed | tf_op | source)
XLA Modules:
  0.0 983.4 jit_solution(1470866713711004327)
XLA Ops:
  6.6 0.7 all-gather.2.cloned.1.call-update
  7.3 0.2 copy-done
  7.5 3.6 fusion.11
  11.1 0.1 fusion.10
  11.2 0.8 broadcast_compare_fusion
  11.9 1.0 fusion.3
  12.9 0.1 multiply_select_fusion
  13.0 0.1 stack.19
  13.1 0.6 fusion.5
  13.7 0.1 stack.18
  13.8 0.2 copy_dynamic-update-slice_fusion.1
  14.0 0.2 copy_dynamic-update-slice_fusion
  14.2 0.3 copy.32
  14.5 1.1 copy.33
  15.6 5.1 all-to-all-start
  20.7 18.7 %fusion.12 = f32[1024,2816]{1,0:T(8,128)} fusion(bf16[1024,2048]{1,0:T(8,128)(2,1)} %param.10, bf16[2048,2816]{1,0:T(8,128)(2,1)} %param.15), kind=kOutput, calls=%fused_computation.28 | convolution fusion | flops 11811160064 | bytes 27262976 | tf_op jit(solution)/shard_map/dot_general | solution.py:19
  39.4 1.1 copy.34
  40.5 5.9 all-to-all-start.1
  46.4 36.3 %fusion.13 = f32[1024,2048]{1,0:T(8,128)} fusion(bf16[2816,2048]{1,0:T(8,128)(2,1)} %param.17, f32[1024,2816]{1,0:T(8,128)} %fusion.12, bf16[1024,2048]{1,0:T(8,128)(2,1)} %param.10, bf16[2048,2816]{1,0:T(8,128)(2,1)} %param.16), kind=kOutput, calls=%fused_computation.29 | convolution fusion | flops 23639621632 | bytes 47185920 | tf_op jit(solution)/shard_map/dot_general | solution.py:22
  82.7 0.8 reshape.25
  83.6 0.1 fusion.9
  83.7 8.0 all-to-all-start.2
  91.7 0.1 fusion.7
  91.8 0.1 pad_maximum_fusion
  91.9 300.7 %all-gather.2.cloned.1.call-done = bf16[32768,2048]{1,0:T(8,128)(2,1)} async-done(((bf16[1024,2048]{1,0:T(8,128)(2,1)}), bf16[32768,2048]{1,0:T(8,128)(2,1)}) %all-gather.2.cloned.1.call-update) | async-done | bytes 134217744 | tf_op jit(solution)/shard_map/all_gather | solution.py:340
  392.7 2.7 copy.35.t_ref
  395.4 0.7 copy-done.3
  396.1 378.5 %experts.1 = (bf16[2,8,2,4,192,1024]{5,4,3,2,1,0:T(8,128)(2,1)}, bf16[16,2,4,192,1024]{4,3,2,1,0:T(8,128)(2,1)}) custom-call(f32[32,2,1024]{2,1,0:T(2,128)} %copy-done.3, bf16[32,1024,2048]{2,1,0:T(8,128)(2,1)} %bitcast.x_ref, bf16[2,2048,1408]{2,1,0:T(8,128)(2,1)} %w1_ref.1, bf16[2,2048,1408]{2,1,0:T(8,128)(2,1)} %w3_ref.1, bf16[2,1408,2048]{2,1,0:T(8,128)(2,1)} %w2_ref.1), custom_call_target="tpu_custom_call" | custom-call | flops 264140488704 | bytes 268435456 | tf_op jit(solution)/shard_map/experts/pallas_call | solution.py:175
  774.6 166.7 %combine.1 = (bf16[2,4,1024,1024]{3,2,1,0:T(8,128)(2,1)}, bf16[8,1024,1024]{2,1,0:T(8,128)(2,1)}) custom-call(f32[2,4,1024,32]{3,2,1,0:T(8,128)} %copy.35.t_ref, bf16[2,8,2,4,192,1024]{5,4,3,2,1,0:T(8,128)(2,1)} %get-tuple-element.13.in_ref), custom_call_target="tpu_custom_call" | custom-call | flops 51539607552 | bytes 50331648 | tf_op jit(solution)/shard_map/combine/pallas_call | solution.py:285
  941.4 18.6 %convert_element_type.12 = f32[2,4,1024,1024]{3,2,1,0:T(8,128)} convert(bf16[2,4,1024,1024]{3,2,1,0:T(8,128)(2,1)} %get-tuple-element.14) | non-fusion elementwise | flops 8388608 | bytes 50331648 | tf_op jit(solution)/shard_map/convert_element_type | solution.py:357
  960.0 13.4 %slice_reduce_fusion.1 = (f32[1024,1024]{1,0:T(8,128)S(1)}, f32[1024,1024]{1,0:T(8,128)S(1)}) fusion(f32[2,4,1024,1024]{3,2,1,0:T(8,128)} %convert_element_type.12), kind=kLoop, calls=%fused_computation.1 | loop fusion | flops 6291456 | bytes 41943040 | tf_op jit(solution)/shard_map/reduce_sum | solution.py:358
  973.4 2.7 fusion
  (10 shorter events, 0.0 us)
Async XLA Ops:
  6.5 1.0 copy-start
  6.6 386.1 %all-gather.2.cloned.1.call-start = ((), (), s32[]{:S(2)}) async-start(), calls=%async_computation.3 | async-start | bytes 138412032 | tf_op jit(solution)/shard_map/all_gather | solution.py:340
  15.6 24.9 %all-to-all-start = ((f32[4,1024,32]{1,2,0:T(8,128)}), f32[4,1024,32]{1,2,0:T(8,128)S(1)}, u32[]{:S(2)}, u32[]{:S(2)}) async-start(f32[4,1024,32]{1,2,0:T(8,128)} %copy.33), calls=%async_computation | async-start | bytes 1048576 | tf_op jit(solution)/shard_map/all_to_all | solution.py:348
  40.5 43.1 %all-to-all-start.1 = ((f32[4,1024,32]{1,2,0:T(8,128)}), f32[4,1024,32]{1,2,0:T(8,128)S(1)}, u32[]{:S(2)}, u32[]{:S(2)}) async-start(f32[4,1024,32]{1,2,0:T(8,128)} %copy.34), calls=%async_computation.1 | async-start | bytes 1048576 | tf_op jit(solution)/shard_map/all_to_all | solution.py:348
  83.7 311.7 %all-to-all-start.2 = ((f32[32,2,1024]{2,1,0:T(2,128)}), f32[32,2,1024]{2,1,0:T(2,128)S(1)}, u32[]{:S(2)}, u32[]{:S(2)}) async-start(f32[32,2,1024]{2,1,0:T(2,128)} %reshape.25), calls=%async_computation.2 | async-start | bytes 524288 | tf_op jit(solution)/shard_map/all_to_all | solution.py:342
  395.4 0.7 copy-start.3
  960.0 13.4 %copy-start.2 = (f32[1024,2048]{1,0:T(8,128)S(1)}, f32[1024,2048]{1,0:T(8,128)}, u32[]{:S(2)}) copy-start(f32[1024,2048]{1,0:T(8,128)} %fusion.13) | copy-start | bytes 25165828
  960.0 16.1 %copy-start.1 = (bf16[2048,64]{0,1:T(8,128)(2,1)S(1)}, bf16[2048,64]{0,1:T(8,128)(2,1)}, u32[]{:S(2)}) copy-start(bf16[2048,64]{0,1:T(8,128)(2,1)} %param.11) | copy-start | bytes 786436
Sparse Core Ops, SparseCore 0:
  9.4 383.2 all-gather.1

commit v3 on v2

--- a/solution.py
+++ b/solution.py
@@ -35,8 +35,72 @@
     return (lax.rem(y, side) * side + lax.rem(x, side)) * CORES + lax.rem(k, CORES)
 
 
-def expert_kernel(side, cap, tab_ref, x_ref, w1_ref, w3_ref, w2_ref, recv, stage, xbuf, rows, act, tail, tile,
-                  x_sem, stage_sem, send_a, recv_a, send_b, recv_b, self_sem):
+def far_first(turn, side):
+    g = lax.rem(turn + 1, side)
+    return lax.rem(2 * g, side - 1) + (side - 1) * (g // (side - 1))
+
+
+def pick_rows(rank, x, cap):
+    hit = rank == lax.broadcasted_iota(jnp.int32, (cap, x.shape[0]), 0).astype(jnp.float32)
+    return dot32(jnp.where(hit, 1.0, 0.0).astype(jnp.bfloat16), x).astype(jnp.bfloat16)
+
+
+def fill_tail(tail, w1_ref, w3_ref):
+    rest = tail.shape[1] // 2
+    full = w1_ref.shape[2] - rest
+    tail[:, :rest] = w1_ref[0, :, full:]
+    tail[:, rest:] = w3_ref[0, :, full:]
+
+
+def partial_kernel(cap, tab_ref, x_ref, w1_ref, w3_ref, o_ref, rows, tail):
+    which, turn = pl.program_id(0), pl.program_id(1)
+    per = x_ref.shape[0]
+    full = w1_ref.shape[2] // COL * COL
+
+    @pl.when(turn == 0)
+    def _():
+        fill_tail(tail, w1_ref, w3_ref)
+
+    @pl.loop(0, per)
+    def _(j):
+        rank = tab_ref[turn * per + j, pl.ds(which, 1), :]
+        rows[pl.ds(pl.multiple_of(j * cap, cap), cap), :] = pick_rows(rank, x_ref[j], cap)
+
+    tok = rows[...]
+    for c in range(0, full, COL):
+        o_ref[0, :, :, c:c + COL] = dot32(tok, w1_ref[0, :, c:c + COL]).reshape(per, cap, COL)
+        o_ref[0, :, :, full + c:full + c + COL] = dot32(tok, w3_ref[0, :, c:c + COL]).reshape(per, cap, COL)
+    o_ref[0, :, :, 2 * full:] = dot32(tok, tail[...]).reshape(per, cap, tail.shape[1])
+
+
+def partial_call(side, cap, tab, x_part, w1, w3):
+    blocks, tokens, part = x_part.shape
+    experts, _, ff = w1.shape
+    once = pl.Buffered(1)
+    return pl.pallas_call(
+        functools.partial(partial_kernel, cap),
+        grid=(experts, blocks // side),
+        in_specs=[
+            pl.BlockSpec(tab.shape, lambda e, t: (0, 0, 0), pipeline_mode=once),
+            pl.BlockSpec((side, tokens, part), lambda e, t: (t, 0, 0)),
+            pl.BlockSpec((1, part, ff), lambda e, t: (e, 0, 0), pipeline_mode=once),
+            pl.BlockSpec((1, part, ff), lambda e, t: (e, 0, 0), pipeline_mode=once),
+        ],
+        out_specs=pl.BlockSpec((1, side, cap, 2 * ff), lambda e, t: (e, t, 0, 0)),
+        out_shape=jax.ShapeDtypeStruct((experts, blocks, cap, 2 * ff), jnp.float32),
+        scratch_shapes=[
+            pltpu.VMEM((side * cap, part), jnp.bfloat16),
+            pltpu.VMEM((part, 2 * (ff % COL)), jnp.bfloat16),
+        ],
+        compiler_params=pltpu.CompilerParams(dimension_semantics=("arbitrary", "arbitrary"), vmem_limit_bytes=VMEM_LIMIT),
+        cost_estimate=pl.CostEstimate(
+            flops=2 * experts * blocks * cap * part * (2 * ff + tokens), bytes_accessed=6 * x_part.size, transcendentals=0),
+        name="partial_products",
+    )(tab, x_part, w1, w3)
+
+
+def expert_kernel(side, cap, tab_ref, x_ref, h_ref, w1_ref, w3_ref, w2_ref, recv, stage, xbuf, hbuf, rows, act, tail, tile,
+                  x_sem, h_sem, stage_sem, send_a, recv_a, send_b, recv_b, self_sem):
     which, turn = pl.program_id(0), pl.program_id(1)
     turns = pl.num_programs(1)
     step = which * turns + turn
@@ -44,17 +108,22 @@
     ff = w1_ref.shape[2]
     full = ff // COL * COL
     rest = ff - full
-    tokens, dim = x_ref.shape[1], x_ref.shape[2]
+    dim = w2_ref.shape[2]
     half = dim // 2
     x, y, k = place(side)
 
     def offsets(s):
         i = lax.rem(s, turns)
-        return s // turns, lax.rem(i // CORES + 1, side), lax.rem(i + 1, CORES)
+        return s // turns, far_first(i // CORES, side), lax.rem(i + 1, CORES)
 
     def fetch(s, j):
         _, dy, dc = offsets(s)
         return pltpu.make_async_copy(x_ref.at[device(side, x + j, y + dy, k + dc)], xbuf.at[j], x_sem.at[j])
+
+    def fetch_h(s, j):
+        e, dy, dc = offsets(s)
+        return pltpu.make_async_copy(
+            h_ref.at[e, device(side, x + j, y + dy, k + dc)], hbuf.at[pl.ds(j * cap, cap)], h_sem.at[j])
 
     def to_column(s):
         e, dy, dc = offsets(s)
@@ -90,7 +159,7 @@
         def _():
             act_on(to_row(s, 0))
 
-        for dx in range(1, side):
+        for dx in (side // 2, *range(1, side // 2), *range(side // 2 + 1, side)):
             act_on(to_row(s, dx))
 
     def locals_(s, act_on):
@@ -113,12 +182,12 @@
     def _():
         for j in range(side):
             fetch(0, j).start()
+            fetch_h(0, j).start()
 
     if rest:
         @pl.when(turn == 0)
         def _():
-            tail[:, :rest] = w1_ref[0, :, full:]
-            tail[:, rest:] = w3_ref[0, :, full:]
+            fill_tail(tail, w1_ref, w3_ref)
 
     _, now_y, now_c = offsets(step)
 
@@ -126,9 +195,7 @@
     def _(j):
         fetch(step, j).wait()
         rank = tab_ref[device(side, x + j, y + now_y, k + now_c), pl.ds(which, 1), :]
-        hit = rank == lax.broadcasted_iota(jnp.int32, (cap, tokens), 0).astype(jnp.float32)
-        pick = jnp.where(hit, 1.0, 0.0).astype(jnp.bfloat16)
-        rows[pl.ds(pl.multiple_of(j * cap, cap), cap), :] = dot32(pick, xbuf[j]).astype(jnp.bfloat16)
+        rows[pl.ds(pl.multiple_of(j * cap, cap), cap), :] = pick_rows(rank, xbuf[j], cap)
 
         @pl.when(step + 1 < steps)
         def _():
@@ -137,15 +204,24 @@
     @pl.when(step > 0)
     def _():
         flush(step - 1)
+
+    for j in range(side):
+        fetch_h(step, j).wait()
 
     tok = rows[...]
     for c in range(0, full, COL):
-        h_gate = dot32(tok, w1_ref[0, :, c:c + COL])
-        h_up = dot32(tok, w3_ref[0, :, c:c + COL])
+        h_gate = hbuf[:, c:c + COL] + dot32(tok, w1_ref[0, :, c:c + COL])
+        h_up = hbuf[:, full + c:full + c + COL] + dot32(tok, w3_ref[0, :, c:c + COL])
         act[:, c:c + COL] = (jax.nn.silu(h_gate) * h_up).astype(jnp.bfloat16)
     if rest:
-        h_both = dot32(tok, tail[...])
+        h_both = hbuf[:, 2 * full:] + dot32(tok, tail[...])
         act[:, full:] = (jax.nn.silu(h_both[:, :rest]) * h_both[:, rest:]).astype(jnp.bfloat16)
+
+    @pl.when(step + 1 < steps)
+    def _():
+        for j in range(side):
+            fetch_h(step + 1, j).start()
+
     a = act[...]
     for c in range(0, dim, COL):
         e = dot32(a, w2_ref[0, :, c:c + COL]).astype(jnp.bfloat16)
@@ -164,9 +240,9 @@
             remotes(s, lambda c: c.wait())
 
 
-def expert_call(side, cap, tab, x_all, w1, w3, w2):
-    blocks, tokens, dim = x_all.shape
-    experts, _, ff = w1.shape
+def expert_call(side, cap, tab, x_part, h_part, w1, w3, w2):
+    blocks, tokens, part = x_part.shape
+    experts, dim, ff = w1.shape
     once = pl.Buffered(1)
     turns = side * CORES
     steps = experts * turns
@@ -178,8 +254,9 @@
         in_specs=[
             pl.BlockSpec(tab.shape, lambda e, t: (0, 0, 0), pipeline_mode=once),
             pl.BlockSpec(memory_space=pl.ANY),
-            pl.BlockSpec((1, dim, ff), lambda e, t: (e, 0, 0), pipeline_mode=once),
-            pl.BlockSpec((1, dim, ff), lambda e, t: (e, 0, 0), pipeline_mode=once),
+            pl.BlockSpec(memory_space=pl.ANY),
+            pl.BlockSpec((1, part, ff), lambda e, t: (e, dim // part - 1, 0)),
+            pl.BlockSpec((1, part, ff), lambda e, t: (e, dim // part - 1, 0)),
             pl.BlockSpec((1, ff, dim), lambda e, t: (e, 0, 0), pipeline_mode=once),
         ],
         out_specs=[pl.BlockSpec(memory_space=pl.ANY)] * 2,
@@ -188,19 +265,20 @@
             jax.ShapeDtypeStruct((steps, 2, side, cap, dim // 2), jnp.bfloat16),
         ],
         scratch_shapes=[
-            pltpu.VMEM((side, tokens, dim), jnp.bfloat16),
-            pltpu.VMEM((rows, dim), jnp.bfloat16),
+            pltpu.VMEM((side, tokens, part), jnp.bfloat16),
+            pltpu.VMEM((rows, 2 * ff), jnp.float32),
+            pltpu.VMEM((rows, part), jnp.bfloat16),
             pltpu.VMEM((rows, ff), jnp.bfloat16),
-            pltpu.VMEM((dim, COL), jnp.bfloat16),
+            pltpu.VMEM((part, 2 * (ff % COL)), jnp.bfloat16),
             pltpu.VMEM((2, side, cap, dim // 2), jnp.bfloat16),
-            dma((side,)), dma, dma((steps,)), dma((steps,)), dma((steps, side)), dma((steps, side)), dma((2,)),
+            dma((side,)), dma((side,)), dma, dma((steps,)), dma((steps,)), dma((steps, side)), dma((steps, side)), dma((2,)),
         ],
         compiler_params=pltpu.CompilerParams(
             dimension_semantics=("arbitrary", "arbitrary"), vmem_limit_bytes=VMEM_LIMIT, has_side_effects=True),
         cost_estimate=pl.CostEstimate(
-            flops=2 * experts * blocks * cap * dim * (3 * ff + tokens), bytes_accessed=4 * x_all.size, transcendentals=0),
+            flops=2 * experts * blocks * cap * part * (4 * ff + tokens), bytes_accessed=8 * x_part.size, transcendentals=0),
         name="experts",
-    )(tab, x_all, w1, w3, w2)
+    )(tab, x_part, h_part, w1, w3, w2)
     return recv
 
 
@@ -215,7 +293,7 @@
     x, y, k = place(side)
 
     def offsets(s):
-        return lax.rem(s // 2 + 1, side), lax.rem(s, 2)
+        return far_first(s // 2, side), lax.rem(s, 2)
 
     def send(s):
         rel, h = offsets(s)
@@ -286,8 +364,8 @@
         functools.partial(combine_kernel, side, cap),
         grid=(side, 2),
         in_specs=[
-            pl.BlockSpec((1, 1, tokens, width), lambda r, h: (h, (r + 1) % side, 0, 0)),
-            pl.BlockSpec((1, turns, experts, 1, cap, half), lambda r, h: (h, 0, 0, (r + 1) % side, 0, 0)),
+            pl.BlockSpec((1, 1, tokens, width), lambda r, h: (h, far_first(r, side), 0, 0)),
+            pl.BlockSpec((1, turns, experts, 1, cap, half), lambda r, h: (h, 0, 0, far_first(r, side), 0, 0)),
         ],
         out_specs=[pl.BlockSpec(memory_space=pl.ANY)] * 2,
         out_shape=[
@@ -307,6 +385,34 @@
         name="combine",
     )(table, rows)
     return recv
+
+
+def finish_kernel(sums_ref, y_ref, o_ref):
+    _, sources, _, half = sums_ref.shape
+    for part in range(2):
+        cols = slice(part * half, (part + 1) * half)
+        routed = sums_ref[part, 0].astype(jnp.float32)
+        for i in range(1, sources):
+            routed += sums_ref[part, i].astype(jnp.float32)
+        o_ref[:, cols] = (y_ref[:, cols] + routed).astype(jnp.bfloat16)
+
+
+def finish_call(sums, y):
+    _, sources, tokens, half = sums.shape
+    rows = tokens // 8
+    return pl.pallas_call(
+        finish_kernel,
+        grid=(8,),
+        in_specs=[
+            pl.BlockSpec((2, sources, rows, half), lambda i: (0, 0, i, 0)),
+            pl.BlockSpec((rows, 2 * half), lambda i: (i, 0)),
+        ],
+        out_specs=pl.BlockSpec((rows, 2 * half), lambda i: (i, 0)),
+        out_shape=jax.ShapeDtypeStruct((tokens, 2 * half), jnp.bfloat16),
+        compiler_params=pltpu.CompilerParams(dimension_semantics=("arbitrary",)),
+        cost_estimate=pl.CostEstimate(flops=2 * sums.size, bytes_accessed=3 * sums.size, transcendentals=0),
+        name="finish",
+    )(sums, y)
 
 
 def routing(hidden, w_router, top_idx, keep_mask):
@@ -337,7 +443,9 @@
         experts = w_router.shape[1]
         per_dev = w_gate.shape[0]
         cap = 8 * ((top_k * tokens + 4 * experts - 1) // (4 * experts))
-        x_all = lax.all_gather(hidden, "ep", axis=0, tiled=True).reshape(groups, tokens, dim)
+        half = dim // 2
+        x_low, x_high = (
+            lax.all_gather(h, "ep", axis=0, tiled=True).reshape(groups, tokens, half) for h in (hidden[:, :half], hidden[:, half:]))
         rank, gate = routing(hidden, w_router, top_idx, keep_mask)
         table = lax.all_to_all(rank.T.reshape(groups, per_dev, tokens), "ep", 0, 0, tiled=True)
         here_x, here_y, _ = place(side)
@@ -352,10 +460,9 @@
         by_y = exchange(both.transpose(2, 0, 1, 3, 4), cols_of, here_y)
         pairs = jnp.stack([by_x, by_y])
         y = swiglu(hidden, shared_gate, shared_up, shared_down)
-        x_all, y, pairs = lax.optimization_barrier((x_all, y, pairs))
-        expert_rows = expert_call(side, cap, table, x_all, w_gate, w_up, w_down)
-        sums = combine_call(side, cap, pairs, expert_rows).astype(jnp.float32)
-        routed = jnp.concatenate([jnp.sum(sums[0], axis=0), jnp.sum(sums[1], axis=0)], axis=1)
-        return (y + routed).astype(jnp.bfloat16)
+        partial = partial_call(side, cap, table, x_low, w_gate, w_up)
+        partial, x_high, y, pairs = lax.optimization_barrier((partial, x_high, y, pairs))
+        expert_rows = expert_call(side, cap, table, x_high, partial, w_gate, w_up, w_down)
+        return finish_call(combine_call(side, cap, pairs, expert_rows), y)
 
     return jax.shard_map(device_fn, mesh=mesh, in_specs=(tok_spec, P(), bank_spec, bank_spec, bank_spec, P(), P(), P(), tok_spec, tok_spec), out_specs=tok_spec, check_vma=False)

time: 989 us -> 894 us (0.904)
  waiting for transfers between devices: 302 us -> 195 us
  Pallas kernels: 545 us -> 592 us
  other arithmetic: 36.9 us -> 1.68 us
    pallas_call x0 -> x2, Pallas kernels: none -> 139 us  [the longest x1 127 us: partial_call(): pl.pallas_call(functools.partial(partial_kernel, cap), grid=(experts, blo...]
    all_gather x1 -> x2, waiting for transfers between devices: 301 us -> 185 us  [device_fn(): lax.all_gather(h, 'ep', axis=0, tiled=True).reshape(groups, tokens, half)]
    pallas_call x1, Pallas kernels: 379 us -> 302 us  [expert_call(): pl.pallas_call(functools.partial(expert_kernel, side, cap), grid=(experts...]
    convert_element_type x2 -> x0, other arithmetic: 21.2 us -> none  [the longest x1 18.6 us: device_fn(): sums = combine_call(side, cap, pairs, expert_rows).astype(jnp.float32)]
    pallas_call x1, Pallas kernels: 167 us -> 152 us  [combine_call(): pl.pallas_call(functools.partial(combine_kernel, side, cap), grid=(side,...]
    reduce_sum x1 -> x0, other arithmetic: 13.4 us -> none  [device_fn(): jnp.sum(sums[0], axis=0)]
  transfers between devices with their start and end apart: 4 -> 5, of which waited for: 1 -> 3; matrix products, arithmetic and copies ran while one was open for 7% -> 7% of each run, Pallas kernels for 0% -> 14%
where the time goes in v3:
time: 894 us; the launch traced here: 893 us
  Pallas kernels  592 us (66%)
  waiting for transfers between devices  195 us (22%)
  matrix products  59.2 us (7%)
  starting transfers between devices  18.9 us (2%)
  between operations  13.6 us (2%)
  local copies, waits for them, and re-layouts  12.3 us (1%)
    pallas_call x1, Pallas kernels, expert_call(): pl.pallas_call(functools.partial(expert_kernel, side, cap), grid=(experts...  302 us
    all_gather x2, waiting for transfers between devices, device_fn(): lax.all_gather(h, 'ep', axis=0, tiled=True).reshape(groups, tokens, half)  185 us
    pallas_call x1, Pallas kernels, combine_call(): pl.pallas_call(functools.partial(combine_kernel, side, cap), grid=(side,...  152 us
    pallas_call x1, Pallas kernels, partial_call(): pl.pallas_call(functools.partial(partial_kernel, cap), grid=(experts, blo...  127 us
    dot_general x1, matrix products, swiglu(): return jnp.dot(act_rows, down_w, preferred_element_type=jnp.float32)  36.2 us
    dot_general x1, matrix products, swiglu(): h_gate = jnp.dot(tok_rows, gate_w, preferred_element_type=jnp.float32)  18.8 us
  transfers between devices with their start and end apart: 5, of which 3 were waited for; matrix products, arithmetic and copies ran while one was open for 7% of the time, Pallas kernels for 14%

profile of v3, /device:TPU:97, one launch (start us, length us, event | category | flops | bytes accessed | tf_op | source)
XLA Modules:
  0.0 893.4 jit_solution(14761658408601956453)
XLA Ops:
  6.6 4.7 fusion.10
  11.3 0.1 all-gather.5.cloned.1.call-start
  11.4 0.7 all-gather.5.cloned.1.call-update
  12.2 3.6 fusion.11
  15.8 0.1 fusion.9
  15.9 0.2 fusion.2
  16.1 0.1 multiply_select_fusion
  16.2 0.1 stack.19
  16.3 0.6 fusion.4
  16.9 0.1 stack.18
  17.0 0.2 copy_dynamic-update-slice_fusion.1
  17.1 0.2 copy_dynamic-update-slice_fusion
  17.3 0.3 copy.32
  17.7 1.1 copy.33
  18.8 5.1 all-to-all-start.1
  23.9 18.8 %fusion.12 = f32[1024,2816]{1,0:T(8,128)} fusion(bf16[1024,2048]{1,0:T(8,128)(2,1)} %param.10, bf16[2048,2816]{1,0:T(8,128)(2,1)} %param.15), kind=kOutput, calls=%fused_computation.25 | convolution fusion | flops 11811160064 | bytes 27262976 | tf_op jit(solution)/shard_map/dot_general | solution.py:19
  42.7 1.1 copy.34
  43.8 5.6 all-to-all-start.2
  49.5 36.2 %fusion.13.y_ref = f32[1024,2048]{1,0:T(8,128)} fusion(bf16[2816,2048]{1,0:T(8,128)(2,1)} %param.17, f32[1024,2816]{1,0:T(8,128)} %fusion.12, bf16[1024,2048]{1,0:T(8,128)(2,1)} %param.10, bf16[2048,2816]{1,0:T(8,128)(2,1)} %param.16), kind=kOutput, calls=%fused_computation.26 | convolution fusion | flops 23639621632 | bytes 47185920 | tf_op jit(solution)/shard_map/dot_general | solution.py:22
  85.6 0.8 reshape.25
  86.5 0.1 fusion.8
  86.6 8.1 all-to-all-start
  94.7 0.1 fusion.6
  94.8 1.1 pad_maximum_fusion
  95.8 9.8 %all-to-all-done.tab_ref = f32[32,2,1024]{2,1,0:T(2,128)S(1)} async-done(((f32[32,2,1024]{2,1,0:T(2,128)}), f32[32,2,1024]{2,1,0:T(2,128)S(1)}, u32[]{:S(2)}, u32[]{:S(2)}) %all-to-all-start) | async-done | bytes 262176 | tf_op jit(solution)/shard_map/all_to_all | solution.py:450
  105.7 114.3 %all-gather.3.cloned.1.call-done = bf16[32768,1024]{1,0:T(8,128)(2,1)} async-done(((bf16[1024,1024]{1,0:T(8,128)(2,1)}), bf16[32768,1024]{1,0:T(8,128)(2,1)}) %all-gather.3.cloned.1.call-update) | async-done | bytes 67108880 | tf_op jit(solution)/shard_map/all_gather | solution.py:448
  220.0 126.6 %partial_products.1.h_ref = f32[2,32,192,2816]{3,2,1,0:T(8,128)} custom-call(f32[32,2,1024]{2,1,0:T(2,128)} %copy-done.2, bf16[32,1024,1024]{2,1,0:T(8,128)(2,1)} %bitcast.1.x_ref, bf16[2,2048,1408]{2,1,0:T(8,128)(2,1)} %w1_ref.3, bf16[2,2048,1408]{2,1,0:T(8,128)(2,1)} %w3_ref.3), custom_call_target="tpu_custom_call" | custom-call | flops 96636764160 | bytes 201326592 | tf_op jit(solution)/shard_map/partial_products/pallas_call | solution.py:80
  346.6 70.4 %all-gather.5.cloned.1.call-done = bf16[32768,1024]{1,0:T(8,128)(2,1)} async-done(((bf16[1024,1024]{1,0:T(8,128)(2,1)}), bf16[32768,1024]{1,0:T(8,128)(2,1)}) %all-gather.5.cloned.1.call-update) | async-done | bytes 67108880 | tf_op jit(solution)/shard_map/all_gather | solution.py:448
  417.0 3.7 copy.35.t_ref
  420.7 301.7 %experts.1 = (bf16[2,8,2,4,192,1024]{5,4,3,2,1,0:T(8,128)(2,1)}, bf16[16,2,4,192,1024]{4,3,2,1,0:T(8,128)(2,1)}) custom-call(f32[32,2,1024]{2,1,0:T(2,128)} %copy-done.2, bf16[32,1024,1024]{2,1,0:T(8,128)(2,1)} %bitcast.2.x_ref, f32[2,32,192,2816]{3,2,1,0:T(8,128)} %partial_products.1.h_ref, bf16[2,2048,1408]{2,1,0:T(8,128)(2,1)} %w1_ref.3, ...), custom_call_target="tpu_custom_call" | custom-call | flops 167503724544 | bytes 268435456 | tf_op jit(solution)/shard_map/experts/pallas_call | solution.py:251
  722.4 152.2 %combine.1 = (bf16[2,4,1024,1024]{3,2,1,0:T(8,128)(2,1)}, bf16[8,1024,1024]{2,1,0:T(8,128)(2,1)}) custom-call(f32[2,4,1024,32]{3,2,1,0:T(8,128)} %copy.35.t_ref, bf16[2,8,2,4,192,1024]{5,4,3,2,1,0:T(8,128)(2,1)} %get-tuple-element.14.in_ref), custom_call_target="tpu_custom_call" | custom-call | flops 51539607552 | bytes 50331648 | tf_op jit(solution)/shard_map/combine/pallas_call | solution.py:363
  874.5 12.0 %finish.1 = bf16[1024,2048]{1,0:T(8,128)(2,1)} custom-call(bf16[2,4,1024,1024]{3,2,1,0:T(8,128)(2,1)} %get-tuple-element.15.sums_ref, f32[1024,2048]{1,0:T(8,128)} %fusion.13.y_ref), custom_call_target="tpu_custom_call" | custom-call | flops 16777216 | bytes 25165824 | tf_op jit(solution)/shard_map/finish/pallas_call | solution.py:403
  (15 shorter events, 0.1 us)
Async XLA Ops:
  6.5 5.6 copy-start
  6.6 9.3 %copy-start.3 = (s32[1024,6]{0,1:T(8,128)S(1)}, s32[1024,6]{0,1:T(8,128)}, u32[]{:S(2)}) copy-start(s32[1024,6]{0,1:T(8,128)} %param.19) | copy-start | bytes 73732
  6.6 9.3 %copy-start.4 = (s32[1024,6]{0,1:T(8,128)S(1)}, s32[1024,6]{0,1:T(8,128)}, u32[]{:S(2)}) copy-start(s32[1024,6]{0,1:T(8,128)} %param.18) | copy-start | bytes 73732
  6.6 213.5 %all-gather.3.cloned.1.call-start = ((), (), s32[]{:S(2)}) async-start(), calls=%async_computation.3 | async-start | bytes 69206016 | tf_op jit(solution)/shard_map/all_gather | solution.py:448
  11.3 405.7 %all-gather.5.cloned.1.call-start = ((), (), s32[]{:S(2)}) async-start(), calls=%async_computation.4 | async-start | bytes 69206016 | tf_op jit(solution)/shard_map/all_gather | solution.py:448
  18.8 25.0 %all-to-all-start.1 = ((f32[4,1024,32]{1,2,0:T(8,128)}), f32[4,1024,32]{1,2,0:T(8,128)S(1)}, u32[]{:S(2)}, u32[]{:S(2)}) async-start(f32[4,1024,32]{1,2,0:T(8,128)} %copy.33), calls=%async_computation.1 | async-start | bytes 1048576 | tf_op jit(solution)/shard_map/all_to_all | solution.py:456
  43.8 42.8 %all-to-all-start.2 = ((f32[4,1024,32]{1,2,0:T(8,128)}), f32[4,1024,32]{1,2,0:T(8,128)S(1)}, u32[]{:S(2)}, u32[]{:S(2)}) async-start(f32[4,1024,32]{1,2,0:T(8,128)} %copy.34), calls=%async_computation.2 | async-start | bytes 1048576 | tf_op jit(solution)/shard_map/all_to_all | solution.py:456
  86.6 19.1 %all-to-all-start = ((f32[32,2,1024]{2,1,0:T(2,128)}), f32[32,2,1024]{2,1,0:T(2,128)S(1)}, u32[]{:S(2)}, u32[]{:S(2)}) async-start(f32[32,2,1024]{2,1,0:T(2,128)} %reshape.25), calls=%async_computation | async-start | bytes 524288 | tf_op jit(solution)/shard_map/all_to_all | solution.py:450
  105.7 114.3 %copy-start.2 = (f32[32,2,1024]{2,1,0:T(2,128)}, f32[32,2,1024]{2,1,0:T(2,128)S(1)}, u32[]{:S(2)}) copy-start(f32[32,2,1024]{2,1,0:T(2,128)S(1)} %all-to-all-done.tab_ref) | copy-start | bytes 786436
  874.5 12.0 %copy-start.1 = (bf16[2048,64]{0,1:T(8,128)(2,1)S(1)}, bf16[2048,64]{0,1:T(8,128)(2,1)}, u32[]{:S(2)}) copy-start(bf16[2048,64]{0,1:T(8,128)(2,1)} %param.11) | copy-start | bytes 786436
Sparse Core Ops, SparseCore 0:
  11.5 208.5 all-gather.2
  222.1 194.8 all-gather.4
